TPU v7x, 32 devices: a whole 2x2x4 slice. The times are simulated.
32 devices in a mesh: dp: 2 (over x), tp: 16 (over y, z, core).
Axes of the slice: x: 2, y: 2, z: 4, core: 2. Of those that a mesh axis runs over, the one named last changes fastest.
Arguments:
- x: bfloat16 [4096, 4096], P('dp'), parts along dimension 0
- dy: bfloat16 [4096, 4096], P('dp'), parts along dimension 0
- gate: bfloat16 [4096, 16384], P('dp', 'tp'), parts along dimension 0
- up: bfloat16 [4096, 16384], P('dp', 'tp'), parts along dimension 0
- w_gate: bfloat16 [4096, 16384], P(None, 'tp')
- w_up: bfloat16 [4096, 16384], P(None, 'tp')
- w_down: bfloat16 [16384, 4096], P('tp')
Outputs:
- output 1: bfloat16 [4096, 4096], P('dp'), parts along dimension 0
- output 2: bfloat16 [8192, 16384], P('dp', 'tp'), parts along dimension 0
- output 3: bfloat16 [8192, 16384], P('dp', 'tp'), parts along dimension 0
- output 4: bfloat16 [32768, 4096], P(('dp', 'tp')), parts along dimension 0
There are 2 independent parts. A program takes and returns all parts, laid end to end along the dimension named above; an argument that names none is the same for every part.
All inputs are finite; a program needn't handle non-finite values.
Results may differ from a plain program's by a relative error of at most 0.012.
Values are sent between devices in bfloat16 or wider.
A program may use at most 2 GiB of HBM per device.

v0:
```python
import jax
import jax.numpy as jnp
from jax import lax
from jax.sharding import PartitionSpec as P


def act(gate, up):
    return jax.nn.silu(gate) * up


def solution(mesh):
    def step(x, dy, gate, up, w_gate, w_up, w_down):
        hidden, back = jax.vjp(act, gate.astype(jnp.float32), up.astype(jnp.float32))
        d_hidden = jnp.dot(dy, w_down.T, preferred_element_type=jnp.float32)
        d_gate, d_up = (g.astype(jnp.bfloat16) for g in back(d_hidden))
        term = jnp.dot(d_gate, w_gate.T, preferred_element_type=jnp.float32) + jnp.dot(d_up, w_up.T, preferred_element_type=jnp.float32)
        dx = lax.psum(term.astype(jnp.bfloat16), "tp")
        dw_gate = jnp.dot(x.T, d_gate, preferred_element_type=jnp.float32)
        dw_up = jnp.dot(x.T, d_up, preferred_element_type=jnp.float32)
        dw_down = jnp.dot(hidden.astype(jnp.bfloat16).T, dy, preferred_element_type=jnp.float32)
        return dx, *(g.astype(jnp.bfloat16) for g in (dw_gate, dw_up, dw_down))

    tokens, columns, rows = P("dp", None), P(None, "tp"), P("tp", None)
    return jax.shard_map(
        step,
        mesh=mesh,
        in_specs=(tokens, tokens, P("dp", "tp"), P("dp", "tp"), columns, columns, rows),
        out_specs=(tokens, P("dp", "tp"), P("dp", "tp"), P(("dp", "tp"), None)),
        check_vma=False,
    )
```

profile of v0, /device:TPU:0, one launch (start us, length us, event | category | flops | bytes accessed | tf_op | source)
XLA Modules:
  0.0 411.0 jit_solution(10739380714384820355)
XLA Ops:
  7.2 0.0 all-reduce.2.cloned.1.call-start
  7.2 0.0 copy-start
  7.2 27.8 %fusion.6 = (bf16[2048,1024]{1,0:T(8,128)(2,1)}, f32[2048,1024]{1,0:T(8,128)}) fusion(bf16[2048,1024]{1,0:T(8,128)(2,1)} %param.9, bf16[2048,1024]{1,0:T(8,128)(2,1)} %param.10, bf16[2048,4096]{1,0:T(8,128)(2,1)} %param.8, bf16[1024,4096]{1,0:T(8,128)(2,1)} %param.13), kind=kOutput, calls=%fused_computation.13 | convolution fusion | flops 17207132160 | bytes 46137344 | tf_op jit(solution)/shard_map/dot_general | solution.py:14
  35.0 0.0 copy-done
  35.0 22.9 %fusion.9 = f32[2048,4096]{1,0:T(8,128)} fusion(bf16[2048,1024]{1,0:T(8,128)(2,1)} %get-tuple-element.8, bf16[4096,1024]{1,0:T(8,128)(2,1)S(1)} %copy-done), kind=kOutput, calls=%fused_computation.19 | convolution fusion | flops 17179869184 | bytes 46137344 | tf_op jit(solution)/shard_map/dot_general | solution.py:16
  57.8 31.3 %add_convert_fusion = bf16[2048,4096]{1,0:T(8,128)(2,1)} fusion(f32[2048,4096]{1,0:T(8,128)} %fusion.9, bf16[4096,1024]{1,0:T(8,128)(2,1)} %param.12, f32[2048,1024]{1,0:T(8,128)} %get-tuple-element.9, bf16[2048,1024]{1,0:T(8,128)(2,1)} %param.9), kind=kOutput, calls=%fused_computation | convolution fusion | flops 17211326464 | bytes 71303168 | tf_op jit(solution)/shard_map/dot_general | solution.py:16
  89.2 0.0 all-reduce.2.cloned.1.call-update
  89.2 23.2 %convert_bitcast_fusion.1 = bf16[4096,1024]{0,1:T(8,128)(2,1)} fusion(bf16[2048,1024]{1,0:T(8,128)(2,1)} %get-tuple-element.8, bf16[2048,4096]{1,0:T(8,128)(2,1)} %param.7), kind=kOutput, calls=%fused_computation.15 | convolution fusion | flops 17184063488 | bytes 29360128 | tf_op jit(solution)/shard_map/dot_general | solution.py:18
  112.5 11.9 %copy.11 = bf16[4096,1024]{1,0:T(8,128)(2,1)} copy(bf16[4096,1024]{0,1:T(8,128)(2,1)} %convert_bitcast_fusion.1) | data formatting | bytes 16777216
  124.4 27.7 %convert_bitcast_fusion = bf16[4096,1024]{0,1:T(8,128)(2,1)} fusion(bf16[2048,4096]{1,0:T(8,128)(2,1)} %param.7, f32[2048,1024]{1,0:T(8,128)} %get-tuple-element.9, bf16[2048,1024]{1,0:T(8,128)(2,1)} %param.9), kind=kOutput, calls=%fused_computation.14 | convolution fusion | flops 17198743552 | bytes 37748736 | tf_op jit(solution)/shard_map/dot_general | solution.py:19
  152.1 11.9 %copy.12 = bf16[4096,1024]{1,0:T(8,128)(2,1)} copy(bf16[4096,1024]{0,1:T(8,128)(2,1)} %convert_bitcast_fusion) | data formatting | bytes 16777216
  164.0 27.4 %convolution_convert_fusion = bf16[1024,4096]{1,0:T(8,128)(2,1)} fusion(bf16[2048,4096]{1,0:T(8,128)(2,1)} %param.8, bf16[2048,1024]{1,0:T(8,128)(2,1)} %param.10, bf16[2048,1024]{1,0:T(8,128)(2,1)} %param.9), kind=kOutput, calls=%fused_computation.17 | convolution fusion | flops 17200840704 | bytes 33554432 | tf_op jit(solution)/shard_map/dot_general | solution.py:20
  191.4 198.7 %all-reduce.2.cloned.1.call-done = bf16[2048,4096]{1,0:T(8,128)(2,1)} async-done(((bf16[2048,4096]{1,0:T(8,128)(2,1)}), bf16[2048,4096]{1,0:T(8,128)(2,1)}) %all-reduce.2.cloned.1.call-update) | async-done | bytes 16777232 | tf_op jit(solution)/shard_map/psum | solution.py:17
  390.1 14.1 %copy.14 = bf16[2048,4096]{1,0:T(8,128)(2,1)} copy(bf16[2048,4096]{1,0:T(8,128)(2,1)} %all-reduce.2.cloned.1.call-done) | data formatting | bytes 33554432
Async XLA Ops:
  7.2 383.0 %all-reduce.2.cloned.1.call-start = ((), (), s32[]{:S(2)}) async-start(), calls=%async_computation | async-start | bytes 33554432 | tf_op jit(solution)/shard_map/psum | solution.py:17
  7.2 27.8 %copy-start = (bf16[4096,1024]{1,0:T(8,128)(2,1)S(1)}, bf16[4096,1024]{1,0:T(8,128)(2,1)}, u32[]{:S(2)}) copy-start(bf16[4096,1024]{1,0:T(8,128)(2,1)} %param.11) | copy-start | bytes 25165828
Sparse Core Ops, SparseCore 0:
  89.3 300.7 all-reduce.1
where the time goes:
time: 412 us; the launch traced here: 411 us
  waiting for transfers between devices  199 us (48%)
  matrix products  160 us (39%)
  local copies, waits for them, and re-layouts  37.9 us (9%)
  between operations  14 us (3%)
    psum x1, waiting for transfers between devices, step(): dx = lax.psum(term.astype(jnp.bfloat16), 'tp')  199 us
    unnamed x5, local copies, waits for them, and re-layouts  37.9 us
    dot_general x1, matrix products, step(): jnp.dot(d_up, w_up.T, preferred_element_type=jnp.float32)  31.3 us
    dot_general x1, matrix products, step(): d_hidden = jnp.dot(dy, w_down.T, preferred_element_type=jnp.float32)  27.8 us
    dot_general x1, matrix products, step(): dw_up = jnp.dot(x.T, d_up, preferred_element_type=jnp.float32)  27.7 us
    dot_general x1, matrix products, step(): jnp.dot(hidden.astype(jnp.bfloat16).T, dy, preferred_element_type=jnp.flo...  27.4 us
    dot_general x1, matrix products, step(): dw_gate = jnp.dot(x.T, d_gate, preferred_element_type=jnp.float32)  23.2 us
    dot_general x1, matrix products, step(): jnp.dot(d_gate, w_gate.T, preferred_element_type=jnp.float32)  22.9 us
  transfers between devices with their start and end apart: 1, of which 1 were waited for; matrix products, arithmetic and copies ran while one was open for 25% of the time, Pallas kernels for 0%

commit v1 on v0

v1 whole, which is shorter than its diff:
```python
import functools

import jax
import jax.numpy as jnp
from jax import lax
from jax.experimental import pallas as pl
from jax.experimental.pallas import tpu as pltpu
from jax.sharding import PartitionSpec as P


F32, BF16 = jnp.float32, jnp.bfloat16
NT = (((1,), (1,)), ((), ()))
TN = (((0,), (0,)), ((), ()))
N = 8
CB = 256


def params(mib):
    return pltpu.CompilerParams(vmem_limit_bytes=mib << 20)


def in_hbm(v):
    return pltpu.with_memory_space_constraint(v, pltpu.HBM)


def cost(flops, bytes_accessed):
    return pl.CostEstimate(flops=flops, bytes_accessed=bytes_accessed, transcendentals=0)


def back_kernel(dy, w_down, gate, up, d_gate, d_up, hidden):
    d_hidden = lax.dot_general(dy[...], w_down[...], NT, preferred_element_type=F32)
    g, u = gate[...].astype(F32), up[...].astype(F32)
    s = jax.nn.sigmoid(g)
    a = g * s
    hidden[...] = (a * u).astype(BF16)
    d_up[...] = (d_hidden * a).astype(BF16)
    d_gate[...] = (d_hidden * u * (s + a * (1.0 - s))).astype(BF16)


def back(dy, w_down, gate, up, tile=1024, tf=256):
    (rows, d), f = dy.shape, gate.shape[1]
    wide = pl.BlockSpec((tile, tf), lambda i, j: (i, j))
    return pl.pallas_call(
        back_kernel,
        grid=(rows // tile, f // tf),
        in_specs=[pl.BlockSpec((tile, d), lambda i, j: (i, 0)), pl.BlockSpec((tf, d), lambda i, j: (j, 0)), wide, wide],
        out_specs=[wide] * 3,
        out_shape=[jax.ShapeDtypeStruct(gate.shape, BF16)] * 3,
        compiler_params=params(30),
        cost_estimate=cost(2 * rows * d * f, 2 * (rows * d + d * f + 5 * rows * f)),
    )(dy, w_down, gate, up)


ANY = pl.BlockSpec(memory_space=pl.ANY)


def column(place, offset, core):
    return lax.rem(place[0] + (offset + N), N) * 2 + core


def pick(offsets, k):
    o = offsets[-1]
    for i in range(len(offsets) - 1):
        o = jnp.where(k == i, offsets[i], o)
    return o


def term_kernel(place, dg, du, wg, wu, *rest):
    out = rest[-1]
    part = 1024

    @pl.loop(0, out.shape[0] // part)
    def _(i):
        r = pl.ds(pl.multiple_of(i * part, part), part)
        t = lax.dot_general(dg[r, :], wg[...], NT, preferred_element_type=F32)
        t = t + lax.dot_general(du[r, :], wu[...], NT, preferred_element_type=F32)
        out[r, :] = t.astype(out.dtype)


def terms(mine, place, offsets, dg, du, wg, wu, after=()):
    nb = len(offsets)
    rows, f = dg.shape
    lhs = pl.BlockSpec((rows, f), lambda j, p: (0, 0), pipeline_mode=pl.Buffered(1))
    rhs = pl.BlockSpec((CB, f), lambda j, p: (column(p, pick(offsets, j), p[1] if mine else 1 - p[1]), 0))
    return pl.pallas_call(
        term_kernel,
        grid_spec=pltpu.PrefetchScalarGridSpec(
            num_scalar_prefetch=1,
            grid=(nb,),
            in_specs=[lhs, lhs, rhs, rhs] + [ANY] * len(after),
            out_specs=pl.BlockSpec((rows, CB), lambda j, p: (0, j)),
        ),
        out_shape=jax.ShapeDtypeStruct((rows, nb * CB), F32 if mine else BF16),
        compiler_params=params(20),
        cost_estimate=cost(4 * nb * rows * CB * f, 4 * (rows + nb * CB) * f + 4 * rows * nb * CB),
    )(place, dg, du, wg, wu, *after)


def add_kernel(only, place, *refs):
    out = refs[-1]
    total = refs[0][...] + refs[1][...].astype(F32)
    for r in refs[2:-1]:
        v = r[...].astype(F32)
        total = total + (v if only is None else jnp.where(place[1] == only, v, jnp.zeros_like(v)))
    out[...] = total.astype(BF16)


def add(place, own, other, k, *got, only=None, tile=512):
    rows = own.shape[0]
    strip = pl.BlockSpec((tile, CB), lambda i, p: (i, k))
    piece = pl.BlockSpec((tile, CB), lambda i, p: (i, 0))
    return pl.pallas_call(
        functools.partial(add_kernel, only),
        grid_spec=pltpu.PrefetchScalarGridSpec(
            num_scalar_prefetch=1, grid=(rows // tile,), in_specs=[strip, strip] + [piece] * len(got), out_specs=piece
        ),
        out_shape=jax.ShapeDtypeStruct((rows, CB), BF16),
        compiler_params=params(8),
        cost_estimate=cost(2 * rows * CB, (8 + 2 * len(got)) * rows * CB),
    )(place, own, other, *got)


class Placing:
    def __init__(self, pieces, where):
        self.pieces, self.where = list(pieces), list(where)
        self.n = len(self.pieces)
        rows = self.pieces[0].shape[0] if self.n else 0
        self.scratch = (
            [pltpu.VMEM((self.n, rows, CB), BF16), pltpu.SemaphoreType.DMA((self.n,)), pltpu.SemaphoreType.DMA((self.n,))]
            if self.n
            else []
        )

    def run(self, step, steps, place, pieces, out, held, load, store):
        loads = [pltpu.make_async_copy(pieces[i], held.at[i], load.at[i]) for i in range(self.n)]
        stores = []
        for i, (o, mine) in enumerate(self.where):
            c = column(place, o, place[1] if mine else 1 - place[1])
            to = out.at[:, pl.ds(pl.multiple_of(c * CB, CB), CB)]
            stores.append(pltpu.make_async_copy(held.at[i], to, store.at[i]))

        @pl.when(step == 0)
        def _():
            for c in loads:
                c.start()

        @pl.when(step == min(1, steps - 1))
        def _():
            for a, b in zip(loads, stores):
                a.wait()
                b.start()

        @pl.when(step == steps - 1)
        def _():
            for c in stores:
                c.wait()


def weights_kernel(kind, steps, extra, placing, place, *refs):
    n = placing.n
    a = refs[: 3 if kind == "pair" else 2]
    pieces = refs[len(a) : len(a) + n]
    outs = refs[len(a) + n + extra :]
    step = pl.program_id(0)
    if n:
        placing.run(step, steps, place, pieces, outs[-4], *outs[-3:])
    if kind == "pair":
        x, dg, du = a
        outs[0][...] = lax.dot_general(x[...], dg[...], TN, preferred_element_type=F32).astype(BF16)
        outs[1][...] = lax.dot_general(x[...], du[...], TN, preferred_element_type=F32).astype(BF16)
    elif kind == "down":
        h, dy = a
        part = 512

        @pl.loop(0, h.shape[1] // part)
        def _(i):
            r = pl.ds(pl.multiple_of(i * part, part), part)
            outs[0][r, :] = lax.dot_general(h[:, r], dy[...], TN, preferred_element_type=F32).astype(BF16)


def weights(kind, place, a, first, count, before=(), dx=None, pieces=(), where=(), after=()):
    placing = Placing(pieces, where)
    tm = 512
    rows, f = a[1].shape if kind == "pair" else a[0].shape
    d = a[0].shape[1] if kind == "pair" else a[1].shape[1]
    whole = pl.BlockSpec((rows, f), lambda i, p: (0, 0), pipeline_mode=pl.Buffered(1))
    tile = pl.BlockSpec((rows, tm), lambda i, p: (0, first + i))
    if kind == "pair":
        ins, outs = [tile, whole, whole], [pl.BlockSpec((tm, f), lambda i, p: (first + i, 0))] * 2
        shapes = [jax.ShapeDtypeStruct((d, f), BF16)] * 2
    else:
        ins, outs = [whole, tile], [pl.BlockSpec((f, tm), lambda i, p: (0, first + i))]
        shapes = [jax.ShapeDtypeStruct((f, d), BF16)]
    given, after = [in_hbm(v) for v in before], [in_hbm(v) for v in after]
    if placing.n:
        given += [] if dx is None else [in_hbm(dx)]
        outs, shapes = outs + [ANY], shapes + [jax.ShapeDtypeStruct((rows, d), BF16)]
    at = 1 + len(ins) + placing.n
    alias = {at + i: i for i in range(len(before))}
    if placing.n and dx is not None:
        alias[at + len(before)] = len(shapes) - 1
    return pl.pallas_call(
        functools.partial(weights_kernel, kind, count, len(given) + len(after), placing),
        grid_spec=pltpu.PrefetchScalarGridSpec(
            num_scalar_prefetch=1,
            grid=(count,),
            in_specs=ins + [ANY] * (placing.n + len(given) + len(after)),
            out_specs=outs,
            scratch_shapes=placing.scratch,
        ),
        out_shape=shapes,
        input_output_aliases=alias,
        compiler_params=params((23 if kind == "pair" else 14) + placing.n),
        cost_estimate=cost(
            len(shapes[: 2 if kind == "pair" else 1]) * 2 * rows * tm * count * f,
            2 * (rows * tm * count + 2 * rows * f + 2 * tm * count * f),
        ),
    )(place, *a, *pieces, *given, *after)


def place_kernel(placing, extra, place, *refs):
    outs = refs[placing.n + extra :]
    placing.run(jnp.int32(0), 1, place, refs[: placing.n], outs[0], *outs[1:])


def put(place, dx, pieces, where):
    placing = Placing(pieces, where)
    n = placing.n
    return pl.pallas_call(
        functools.partial(place_kernel, placing, 1),
        grid_spec=pltpu.PrefetchScalarGridSpec(
            num_scalar_prefetch=1, grid=(), in_specs=[ANY] * (n + 1), out_specs=ANY, scratch_shapes=placing.scratch
        ),
        out_shape=jax.ShapeDtypeStruct(dx.shape, BF16),
        input_output_aliases={1 + n: 0},
        compiler_params=params(14),
        cost_estimate=cost(n * dx.shape[0] * CB, 4 * n * dx.shape[0] * CB),
    )(place, *pieces, dx)


def ring_order():
    def chip(p):
        p %= N
        return p if p < 4 else 4 + (N - 1 - p)

    return lambda p, c: chip(p) * 2 + c


def solution(mesh):
    dev = ring_order()
    right = [(dev(p, c), dev(p + 1, c)) for p in range(N) for c in (0, 1)]
    left = [(dev(p, c), dev(p - 1, c)) for p in range(N) for c in (0, 1)]
    apart = [(dev(p, c), dev(p + 1 - 2 * c, c)) for p in range(N) for c in (0, 1)]
    swap = [(dev(p, c), dev(p, 1 - c)) for p in range(N) for c in (0, 1)]

    def send(v, pairs):
        return lax.ppermute(v, "tp", pairs)

    def step(x, dy, gate, up, w_gate, w_up, w_down):
        index = lax.axis_index("tp")
        core, chip = index % 2, index // 2
        place = jnp.stack([jnp.where(chip < 4, chip, N + 3 - chip), core]).astype(jnp.int32)
        x, dy, gate, up, w_gate, w_up, w_down = (
            in_hbm(v) for v in (x, dy, gate, up, w_gate, w_up, w_down)
        )
        d_gate, d_up, hidden = back(dy, w_down, gate, up)
        hidden = in_hbm(hidden)
        d_gate, d_up = (pltpu.with_memory_space_constraint(v, pltpu.VMEM) for v in (d_gate, d_up))

        def stage(o, *after):
            given = (place, o, d_gate, d_up, w_gate, w_up, after)
            other = terms(False, *given)
            other = send(other, swap)
            return other, terms(True, *given)

        def gradients(kind, first, count, *more):
            given = (hidden, dy) if kind == "down" else (x, d_gate, d_up)
            return weights(kind, place, given, first, count, *more)

        def both(v):
            return [(-v, True), (v, True)], [(-v, False), (v, False)]

        other, own = stage((4,))
        far = add(place, own, other, 0)
        other, own = stage((3, -3), far)
        dw_down = ()
        got_r = got_l = send(far, apart)
        for o, then in ((3, (2, -2)), (2, (1, -1)), (1, (0,))):
            to_r = add(place, own, other, 0, got_r, only=0 if o == 3 else None)
            to_l = add(place, own, other, 1, got_l, only=1 if o == 3 else None)
            other, own = stage(then, to_r, to_l)
            got_r, got_l = send(to_r, right), send(to_l, left)
            first, count = {3: (0, 1), 2: (1, 1), 1: (2, 2)}[o]
            dw_down = gradients("down", first, count, dw_down)
        done = add(place, own, other, 0, got_r, got_l)

        a1 = [send(done, right), send(done, left)]
        b0 = [send(done, swap)]
        *dw, dx = gradients("pair", 0, 3, (), None, [done], [(0, True)])
        a2 = [send(a1[0], right), send(a1[1], left)]
        b1 = [send(v, swap) for v in a1]
        *dw, dx = gradients("pair", 3, 3, dw, dx, b0 + a1, [(0, False)] + both(1)[0])
        a3 = [send(a2[0], right), send(a2[1], left)]
        b2 = [send(v, swap) for v in a2]
        *dw, dx = gradients("pair", 6, 2, dw, dx, b1 + a2, both(1)[1] + both(2)[0])
        dw_down = gradients("down", 4, 1, dw_down, None, (), (), (dx,))
        last = send(jnp.where(core == 0, a3[0], a3[1]), apart)
        b3 = [send(v, swap) for v in a3]
        dw_down, dx = gradients("down", 5, 3, dw_down, dx, b2 + a3, both(2)[1] + both(3)[0])
        dx = put(place, dx, b3, both(3)[1])
        dx = put(place, dx, [last, send(last, swap)], [(4, True), (4, False)])
        return dx, *dw, dw_down

    tokens, columns, rows = P("dp", None), P(None, "tp"), P("tp", None)
    return jax.shard_map(
        step,
        mesh=mesh,
        in_specs=(tokens, tokens, P("dp", "tp"), P("dp", "tp"), columns, columns, rows),
        out_specs=(tokens, P("dp", "tp"), P("dp", "tp"), P(("dp", "tp"), None)),
        check_vma=False,
    )
```

time: 412 us -> 305 us (0.74)
  Pallas kernels: 0 us -> 196 us
  matrix products: 160 us -> 0 us
  waiting for transfers between devices: 199 us -> 87.2 us
  local copies, waits for them, and re-layouts: 37.9 us -> 0.03 us
  starting transfers between devices: 0.04 us -> 19.7 us
  between operations: 14 us -> 1.18 us
    psum x1 -> x0, waiting for transfers between devices: 199 us -> none  [step(): dx = lax.psum(term.astype(jnp.bfloat16), 'tp')]
    pallas_call x0 -> x29, Pallas kernels: none -> 196 us  [the longest x8 93 us: weights(): pl.pallas_call(functools.partial(weights_kernel, kind, count, len(given)...]
    dot_general x6 -> x0, matrix products: 160 us -> none  [the longest x1 31.3 us: step(): jnp.dot(d_up, w_up.T, preferred_element_type=jnp.float32)]
    ppermute x0 -> x27, waiting for transfers between devices: none -> 87.2 us  [send(): return lax.ppermute(v, 'tp', pairs)]
    unnamed x5 -> x14, local copies, waits for them, and re-layouts: 37.9 us -> 0.03 us
    ppermute x0 -> x27, starting transfers between devices: none -> 19.7 us  [send(): return lax.ppermute(v, 'tp', pairs)]
  transfers between devices with their start and end apart: 1 -> 27, of which waited for: 1 -> 10; matrix products, arithmetic and copies ran while one was open for 25% -> 0% of each run, Pallas kernels for 0% -> 42%
where the time goes in v1:
time: 305 us; the launch traced here: 304 us
  Pallas kernels  196 us (64%)
  waiting for transfers between devices  87.2 us (29%)
  starting transfers between devices  19.7 us (6%)
    pallas_call x8, Pallas kernels, weights(): pl.pallas_call(functools.partial(weights_kernel, kind, count, len(given)...  93 us
    ppermute x27, waiting for transfers between devices, send(): return lax.ppermute(v, 'tp', pairs)  87.2 us
    pallas_call x10, Pallas kernels, terms(): pl.pallas_call(term_kernel, grid_spec=pltpu.PrefetchScalarGridSpec(num_sc...  61.5 us
    pallas_call x1, Pallas kernels, back(): pl.pallas_call(back_kernel, grid=(rows // tile, f // tf), in_specs=[pl.Bl...  28.5 us
    ppermute x27, starting transfers between devices, send(): return lax.ppermute(v, 'tp', pairs)  19.7 us
    pallas_call x8, Pallas kernels, add(): pl.pallas_call(functools.partial(add_kernel, only), grid_spec=pltpu.Prefe...  9.06 us
  transfers between devices with their start and end apart: 27, of which 10 were waited for; matrix products, arithmetic and copies ran while one was open for 0% of the time, Pallas kernels for 42%

profile of v1, /device:TPU:0, one launch (start us, length us, event | category | flops | bytes accessed | tf_op | source)
XLA Modules:
  0.0 304.4 jit_solution(6229712173204784420)
XLA Ops:
  0.7 28.5 %shard_map.102 = (bf16[2048,1024]{1,0:T(8,128)(2,1)S(1)}, bf16[2048,1024]{1,0:T(8,128)(2,1)S(1)}, bf16[2048,1024]{1,0:T(8,128)(2,1)S(1)}) custom-call(bf16[2048,4096]{1,0:T(8,128)(2,1)} %refs_1_.9, bf16[1024,4096]{1,0:T(8,128)(2,1)} %w_down.1, bf16[2048,1024]{1,0:T(8,128)(2,1)} %gate.1, bf16[2048,1024]{1,0:T(8,128)(2,1)} %up.1), custom_call_target="tpu_custom_call" | custom-call | flops 17179869184 | bytes 46137344 | tf_op jit(solution)/shard_map/pallas_call | solution.py:43
  29.3 5.1 %shard_map.104 = bf16[2048,256]{1,0:T(8,128)(2,1)S(1)} custom-call(s32[2]{0:T(128)S(1)} %pad_add_fusion.place, bf16[2048,1024]{1,0:T(8,128)(2,1)S(1)} %get-tuple-element.18.dg.refs_1_, bf16[2048,1024]{1,0:T(8,128)(2,1)S(1)} %get-tuple-element.19.du.refs_2_, bf16[4096,1024]{1,0:T(8,128)(2,1)} %wg.19, bf16[4096,1024]{1,0:T(8,128)(2,1)} %wu.19), custom_call_target="tpu_custom_call" | custom-call | flops 2147483648 | bytes 11534336 | tf_op jit(solution)/shard_map/pallas_call | solution.py:85
  40.1 7.1 %shard_map.107 = bf16[2048,512]{1,0:T(8,128)(2,1)S(1)} custom-call(s32[2]{0:T(128)S(1)} %pad_add_fusion.place, bf16[2048,1024]{1,0:T(8,128)(2,1)S(1)} %get-tuple-element.18.dg.refs_1_, bf16[2048,1024]{1,0:T(8,128)(2,1)S(1)} %get-tuple-element.19.du.refs_2_, bf16[4096,1024]{1,0:T(8,128)(2,1)} %wg.19, bf16[4096,1024]{1,0:T(8,128)(2,1)} %wu.19, ...), custom_call_target="tpu_custom_call" | custom-call | flops 4294967296 | bytes 14680064 | tf_op jit(solution)/shard_map/pallas_call | solution.py:85
  50.4 7.3 %shard_map.106.refs_0_ = f32[2048,512]{1,0:T(8,128)S(1)} custom-call(s32[2]{0:T(128)S(1)} %pad_add_fusion.place, bf16[2048,1024]{1,0:T(8,128)(2,1)S(1)} %get-tuple-element.18.dg.refs_1_, bf16[2048,1024]{1,0:T(8,128)(2,1)S(1)} %get-tuple-element.19.du.refs_2_, bf16[4096,1024]{1,0:T(8,128)(2,1)} %wg.19, bf16[4096,1024]{1,0:T(8,128)(2,1)} %wu.19, ...), custom_call_target="tpu_custom_call" | custom-call | flops 4294967296 | bytes 14680064 | tf_op jit(solution)/shard_map/pallas_call | solution.py:85
  57.7 5.4 %collective-permute-done.2.refs_2_ = bf16[2048,256]{1,0:T(8,128)(2,1)S(1)} collective-permute-done((bf16[2048,256]{1,0:T(8,128)(2,1)S(1)}, bf16[2048,256]{1,0:T(8,128)(2,1)S(1)}, u32[]{:S(2)}, u32[]{:S(2)}) %collective-permute-start.2) | collective-permute-done | bytes 1048608 | tf_op jit(solution)/shard_map/ppermute | solution.py:257
  65.6 7.2 %shard_map.111 = bf16[2048,512]{1,0:T(8,128)(2,1)S(1)} custom-call(s32[2]{0:T(128)S(1)} %pad_add_fusion.place, bf16[2048,1024]{1,0:T(8,128)(2,1)S(1)} %get-tuple-element.18.dg.refs_1_, bf16[2048,1024]{1,0:T(8,128)(2,1)S(1)} %get-tuple-element.19.du.refs_2_, bf16[4096,1024]{1,0:T(8,128)(2,1)} %wg.19, bf16[4096,1024]{1,0:T(8,128)(2,1)} %wu.19, ...), custom_call_target="tpu_custom_call" | custom-call | flops 4294967296 | bytes 14680064 | tf_op jit(solution)/shard_map/pallas_call | solution.py:85
  75.0 7.3 %shard_map.110.refs_0_ = f32[2048,512]{1,0:T(8,128)S(1)} custom-call(s32[2]{0:T(128)S(1)} %pad_add_fusion.place, bf16[2048,1024]{1,0:T(8,128)(2,1)S(1)} %get-tuple-element.18.dg.refs_1_, bf16[2048,1024]{1,0:T(8,128)(2,1)S(1)} %get-tuple-element.19.du.refs_2_, bf16[4096,1024]{1,0:T(8,128)(2,1)} %wg.19, bf16[4096,1024]{1,0:T(8,128)(2,1)} %wu.19, ...), custom_call_target="tpu_custom_call" | custom-call | flops 4294967296 | bytes 14680064 | tf_op jit(solution)/shard_map/pallas_call | solution.py:85
  82.3 16.4 %collective-permute-done.5.refs_2_ = bf16[2048,256]{1,0:T(8,128)(2,1)S(1)} collective-permute-done((bf16[2048,256]{1,0:T(8,128)(2,1)S(1)}, bf16[2048,256]{1,0:T(8,128)(2,1)S(1)}, u32[]{:S(2)}, u32[]{:S(2)}) %collective-permute-start.5) | collective-permute-done | bytes 1048608 | tf_op jit(solution)/shard_map/ppermute | solution.py:257
  101.3 7.1 %shard_map.115 = bf16[2048,512]{1,0:T(8,128)(2,1)S(1)} custom-call(s32[2]{0:T(128)S(1)} %pad_add_fusion.place, bf16[2048,1024]{1,0:T(8,128)(2,1)S(1)} %get-tuple-element.18.dg.refs_1_, bf16[2048,1024]{1,0:T(8,128)(2,1)S(1)} %get-tuple-element.19.du.refs_2_, bf16[4096,1024]{1,0:T(8,128)(2,1)} %wg.19, bf16[4096,1024]{1,0:T(8,128)(2,1)} %wu.19, ...), custom_call_target="tpu_custom_call" | custom-call | flops 4294967296 | bytes 14680064 | tf_op jit(solution)/shard_map/pallas_call | solution.py:85
  110.6 7.3 %shard_map.114.refs_0_ = f32[2048,512]{1,0:T(8,128)S(1)} custom-call(s32[2]{0:T(128)S(1)} %pad_add_fusion.place, bf16[2048,1024]{1,0:T(8,128)(2,1)S(1)} %get-tuple-element.18.dg.refs_1_, bf16[2048,1024]{1,0:T(8,128)(2,1)S(1)} %get-tuple-element.19.du.refs_2_, bf16[4096,1024]{1,0:T(8,128)(2,1)} %wg.19, bf16[4096,1024]{1,0:T(8,128)(2,1)} %wu.19, ...), custom_call_target="tpu_custom_call" | custom-call | flops 4294967296 | bytes 14680064 | tf_op jit(solution)/shard_map/pallas_call | solution.py:85
  117.9 16.2 %collective-permute-done.8.refs_2_ = bf16[2048,256]{1,0:T(8,128)(2,1)S(1)} collective-permute-done((bf16[2048,256]{1,0:T(8,128)(2,1)S(1)}, bf16[2048,256]{1,0:T(8,128)(2,1)S(1)}, u32[]{:S(2)}, u32[]{:S(2)}) %collective-permute-start.8) | collective-permute-done | bytes 1048608 | tf_op jit(solution)/shard_map/ppermute | solution.py:257
  136.6 4.3 %shard_map.119 = bf16[2048,256]{1,0:T(8,128)(2,1)S(1)} custom-call(s32[2]{0:T(128)S(1)} %pad_add_fusion.place, bf16[2048,1024]{1,0:T(8,128)(2,1)S(1)} %get-tuple-element.18.dg.refs_1_, bf16[2048,1024]{1,0:T(8,128)(2,1)S(1)} %get-tuple-element.19.du.refs_2_, bf16[4096,1024]{1,0:T(8,128)(2,1)} %wg.19, bf16[4096,1024]{1,0:T(8,128)(2,1)} %wu.19, ...), custom_call_target="tpu_custom_call" | custom-call | flops 2147483648 | bytes 11534336 | tf_op jit(solution)/shard_map/pallas_call | solution.py:85
  143.1 4.3 %shard_map.118.refs_0_ = f32[2048,256]{1,0:T(8,128)S(1)} custom-call(s32[2]{0:T(128)S(1)} %pad_add_fusion.place, bf16[2048,1024]{1,0:T(8,128)(2,1)S(1)} %get-tuple-element.18.dg.refs_1_, bf16[2048,1024]{1,0:T(8,128)(2,1)S(1)} %get-tuple-element.19.du.refs_2_, bf16[4096,1024]{1,0:T(8,128)(2,1)} %wg.19, bf16[4096,1024]{1,0:T(8,128)(2,1)} %wu.19, ...), custom_call_target="tpu_custom_call" | custom-call | flops 2147483648 | bytes 11534336 | tf_op jit(solution)/shard_map/pallas_call | solution.py:85
  147.4 19.1 %collective-permute-done.11.refs_3_ = bf16[2048,256]{1,0:T(8,128)(2,1)S(1)} collective-permute-done((bf16[2048,256]{1,0:T(8,128)(2,1)S(1)}, bf16[2048,256]{1,0:T(8,128)(2,1)S(1)}, u32[]{:S(2)}, u32[]{:S(2)}) %collective-permute-start.11) | collective-permute-done | bytes 1048608 | tf_op jit(solution)/shard_map/ppermute | solution.py:257
  171.0 22.5 %collective-permute-done.12.refs_4_ = bf16[2048,256]{1,0:T(8,128)(2,1)} collective-permute-done((bf16[2048,256]{1,0:T(8,128)(2,1)S(1)}, bf16[2048,256]{1,0:T(8,128)(2,1)}, u32[]{:S(2)}, u32[]{:S(2)}) %collective-permute-start.12) | collective-permute-done | bytes 1048608 | tf_op jit(solution)/shard_map/ppermute | solution.py:257
  195.5 7.0 %shard_map.121.refs_2_ = bf16[1024,4096]{1,0:T(8,128)(2,1)} custom-call(s32[2]{0:T(128)S(1)} %pad_add_fusion.place, bf16[2048,1024]{1,0:T(8,128)(2,1)} %copy-done.4, bf16[2048,4096]{1,0:T(8,128)(2,1)} %refs_1_.9), custom_call_target="tpu_custom_call" | custom-call | flops 2147483648 | bytes 12582912 | tf_op jit(solution)/shard_map/pallas_call | solution.py:202
  202.5 6.9 %shard_map.122.refs_2_ = bf16[1024,4096]{1,0:T(8,128)(2,1)} custom-call(s32[2]{0:T(128)S(1)} %pad_add_fusion.place, bf16[2048,1024]{1,0:T(8,128)(2,1)} %copy-done.4, bf16[2048,4096]{1,0:T(8,128)(2,1)} %refs_1_.9, bf16[1024,4096]{1,0:T(8,128)(2,1)} %shard_map.121.refs_2_), custom_call_target="tpu_custom_call", output_to_operand_aliasing={{}: (3, {})} | custom-call | flops 2147483648 | bytes 12582912 | tf_op jit(solution)/shard_map/pallas_call | solution.py:202
  209.4 9.8 %shard_map.123.refs_2_ = bf16[1024,4096]{1,0:T(8,128)(2,1)} custom-call(s32[2]{0:T(128)S(1)} %pad_add_fusion.place, bf16[2048,1024]{1,0:T(8,128)(2,1)} %copy-done.4, bf16[2048,4096]{1,0:T(8,128)(2,1)} %refs_1_.9, bf16[1024,4096]{1,0:T(8,128)(2,1)} %shard_map.122.refs_2_), custom_call_target="tpu_custom_call", output_to_operand_aliasing={{}: (3, {})} | custom-call | flops 4294967296 | bytes 16777216 | tf_op jit(solution)/shard_map/pallas_call | solution.py:202
  221.3 17.0 %shard_map.124 = (bf16[4096,1024]{1,0:T(8,128)(2,1)}, bf16[4096,1024]{1,0:T(8,128)(2,1)}, bf16[2048,4096]{1,0:T(8,128)(2,1)}) custom-call(s32[2]{0:T(128)S(1)} %pad_add_fusion.place, bf16[2048,4096]{1,0:T(8,128)(2,1)} %refs_0_.5, bf16[2048,1024]{1,0:T(8,128)(2,1)S(1)} %copy-done.1, bf16[2048,1024]{1,0:T(8,128)(2,1)S(1)} %copy-done.3, ...), custom_call_target="tpu_custom_call" | custom-call | flops 12884901888 | bytes 20971520 | tf_op jit(solution)/shard_map/pallas_call | solution.py:202
  238.9 5.9 %collective-permute-done.14.refs_4_ = bf16[2048,256]{1,0:T(8,128)(2,1)S(1)} collective-permute-done((bf16[2048,256]{1,0:T(8,128)(2,1)S(1)}, bf16[2048,256]{1,0:T(8,128)(2,1)S(1)}, u32[]{:S(2)}, u32[]{:S(2)}) %collective-permute-start.14) | collective-permute-done | bytes 1048608 | tf_op jit(solution)/shard_map/ppermute | solution.py:257
  246.9 17.2 %shard_map.125 = (bf16[4096,1024]{1,0:T(8,128)(2,1)}, bf16[4096,1024]{1,0:T(8,128)(2,1)}, bf16[2048,4096]{1,0:T(8,128)(2,1)}) custom-call(s32[2]{0:T(128)S(1)} %pad_add_fusion.place, bf16[2048,4096]{1,0:T(8,128)(2,1)} %refs_0_.5, bf16[2048,1024]{1,0:T(8,128)(2,1)S(1)} %copy-done.1, ...), custom_call_target="tpu_custom_call", output_to_operand_aliasing={{0}: (7, {}), {1}: (8, {}), {2}: (9, {})} | custom-call | flops 12884901888 | bytes 20971520 | tf_op jit(solution)/shard_map/pallas_call | solution.py:202
  265.0 15.0 %shard_map.126 = (bf16[4096,1024]{1,0:T(8,128)(2,1)}, bf16[4096,1024]{1,0:T(8,128)(2,1)}, bf16[2048,4096]{1,0:T(8,128)(2,1)}) custom-call(s32[2]{0:T(128)S(1)} %pad_add_fusion.place, bf16[2048,4096]{1,0:T(8,128)(2,1)} %refs_0_.5, bf16[2048,1024]{1,0:T(8,128)(2,1)S(1)} %copy-done.1, ...), custom_call_target="tpu_custom_call", output_to_operand_aliasing={{0}: (8, {}), {1}: (9, {}), {2}: (10, {})} | custom-call | flops 8589934592 | bytes 16777216 | tf_op jit(solution)/shard_map/pallas_call | solution.py:202
  280.0 7.0 %shard_map.127.refs_6_ = bf16[1024,4096]{1,0:T(8,128)(2,1)} custom-call(s32[2]{0:T(128)S(1)} %pad_add_fusion.place, bf16[2048,1024]{1,0:T(8,128)(2,1)} %copy-done.4, bf16[2048,4096]{1,0:T(8,128)(2,1)} %refs_1_.9, bf16[1024,4096]{1,0:T(8,128)(2,1)} %shard_map.123.refs_2_, ...), custom_call_target="tpu_custom_call", output_to_operand_aliasing={{}: (3, {})} | custom-call | flops 2147483648 | bytes 12582912 | tf_op jit(solution)/shard_map/pallas_call | solution.py:202
  286.9 13.1 %shard_map.128 = (bf16[1024,4096]{1,0:T(8,128)(2,1)}, bf16[2048,4096]{1,0:T(8,128)(2,1)}) custom-call(s32[2]{0:T(128)S(1)} %pad_add_fusion.place, bf16[2048,1024]{1,0:T(8,128)(2,1)} %copy-done.4, bf16[2048,4096]{1,0:T(8,128)(2,1)} %refs_1_.9, bf16[2048,256]{1,0:T(8,128)(2,1)S(1)} %collective-permute-done.22.refs_2_, ...), custom_call_target="tpu_custom_call", output_to_operand_aliasing={{0}: (7, {}), {1}: (8, {})} | custom-call | flops 6442450944 | bytes 20971520 | tf_op jit(solution)/shard_map/pallas_call | solution.py:202
  (75 shorter events, 39.2 us)
Async XLA Ops:
  47.2 15.8 %collective-permute-start.1 = (bf16[2048,512]{1,0:T(8,128)(2,1)S(1)}, bf16[2048,512]{1,0:T(8,128)(2,1)S(1)}, u32[]{:S(2)}, u32[]{:S(2)}) collective-permute-start(bf16[2048,512]{1,0:T(8,128)(2,1)S(1)} %shard_map.107), channel_id=1, source_target_pairs={{0,1},{1,0},{2,3},{3,2},{4,5},{5,4},{6,7},{7,6},{14,15},{15,14},{1... | collective-permute-start | bytes 6291464 | tf_op jit(solution)/shard_map/ppermute | solution.py:257
  72.7 26.0 %collective-permute-start.3 = (bf16[2048,512]{1,0:T(8,128)(2,1)S(1)}, bf16[2048,512]{1,0:T(8,128)(2,1)S(1)}, u32[]{:S(2)}, u32[]{:S(2)}) collective-permute-start(bf16[2048,512]{1,0:T(8,128)(2,1)S(1)} %shard_map.111), channel_id=1, source_target_pairs={{0,1},{1,0},{2,3},{3,2},{4,5},{5,4},{6,7},{7,6},{14,15},{15,14},{1... | collective-permute-start | bytes 6291464 | tf_op jit(solution)/shard_map/ppermute | solution.py:257
  72.8 25.9 %collective-permute-start.5 = (bf16[2048,256]{1,0:T(8,128)(2,1)S(1)}, bf16[2048,256]{1,0:T(8,128)(2,1)S(1)}, u32[]{:S(2)}, u32[]{:S(2)}) collective-permute-start(bf16[2048,256]{1,0:T(8,128)(2,1)S(1)} %shard_map.109.rest_1_), channel_id=1, source_target_pairs={{0,8},{1,9},{2,0},{3,1},{4,2},{5,3},{6,4},{7,5},{14,6},{15,7},{12,... | collective-permute-start | bytes 3145736 | tf_op jit(solution)/shard_map/ppermute | solution.py:257
  74.9 25.2 %collective-permute-start.4 = (bf16[2048,256]{1,0:T(8,128)(2,1)S(1)}, bf16[2048,256]{1,0:T(8,128)(2,1)S(1)}, u32[]{:S(2)}, u32[]{:S(2)}) collective-permute-start(bf16[2048,256]{1,0:T(8,128)(2,1)S(1)} %shard_map.108.rest_0_), channel_id=1, source_target_pairs={{0,2},{1,3},{2,4},{3,5},{4,6},{5,7},{6,14},{7,15},{14,12},{15,13},... | collective-permute-start | bytes 3145736 | tf_op jit(solution)/shard_map/ppermute | solution.py:257
  108.4 25.6 %collective-permute-start.6 = (bf16[2048,512]{1,0:T(8,128)(2,1)S(1)}, bf16[2048,512]{1,0:T(8,128)(2,1)S(1)}, u32[]{:S(2)}, u32[]{:S(2)}) collective-permute-start(bf16[2048,512]{1,0:T(8,128)(2,1)S(1)} %shard_map.115), channel_id=1, source_target_pairs={{0,1},{1,0},{2,3},{3,2},{4,5},{5,4},{6,7},{7,6},{14,15},{15,14},{1... | collective-permute-start | bytes 6291464 | tf_op jit(solution)/shard_map/ppermute | solution.py:257
  108.5 25.6 %collective-permute-start.8 = (bf16[2048,256]{1,0:T(8,128)(2,1)S(1)}, bf16[2048,256]{1,0:T(8,128)(2,1)S(1)}, u32[]{:S(2)}, u32[]{:S(2)}) collective-permute-start(bf16[2048,256]{1,0:T(8,128)(2,1)S(1)} %shard_map.113.rest_1_), channel_id=1, source_target_pairs={{0,8},{1,9},{2,0},{3,1},{4,2},{5,3},{6,4},{7,5},{14,6},{15,7},{12,... | collective-permute-start | bytes 3145736 | tf_op jit(solution)/shard_map/ppermute | solution.py:257
  110.2 25.2 %collective-permute-start.7 = (bf16[2048,256]{1,0:T(8,128)(2,1)S(1)}, bf16[2048,256]{1,0:T(8,128)(2,1)S(1)}, u32[]{:S(2)}, u32[]{:S(2)}) collective-permute-start(bf16[2048,256]{1,0:T(8,128)(2,1)S(1)} %shard_map.112.rest_0_), channel_id=1, source_target_pairs={{0,2},{1,3},{2,4},{3,5},{4,6},{5,7},{6,14},{7,15},{14,12},{15,13},... | collective-permute-start | bytes 3145736 | tf_op jit(solution)/shard_map/ppermute | solution.py:257
  141.0 25.6 %collective-permute-start.11 = (bf16[2048,256]{1,0:T(8,128)(2,1)S(1)}, bf16[2048,256]{1,0:T(8,128)(2,1)S(1)}, u32[]{:S(2)}, u32[]{:S(2)}) collective-permute-start(bf16[2048,256]{1,0:T(8,128)(2,1)S(1)} %shard_map.117.rest_1_), channel_id=1, source_target_pairs={{0,8},{1,9},{2,0},{3,1},{4,2},{5,3},{6,4},{7,5},{14,6},{15,7},{12,... | collective-permute-start | bytes 3145736 | tf_op jit(solution)/shard_map/ppermute | solution.py:257
  142.6 25.2 %collective-permute-start.10 = (bf16[2048,256]{1,0:T(8,128)(2,1)S(1)}, bf16[2048,256]{1,0:T(8,128)(2,1)S(1)}, u32[]{:S(2)}, u32[]{:S(2)}) collective-permute-start(bf16[2048,256]{1,0:T(8,128)(2,1)S(1)} %shard_map.116.rest_0_), channel_id=1, source_target_pairs={{0,2},{1,3},{2,4},{3,5},{4,6},{5,7},{6,14},{7,15},{14,12},{15,13},... | collective-permute-start | bytes 3145736 | tf_op jit(solution)/shard_map/ppermute | solution.py:257
  168.9 24.5 %collective-permute-start.12 = (bf16[2048,256]{1,0:T(8,128)(2,1)S(1)}, bf16[2048,256]{1,0:T(8,128)(2,1)}, u32[]{:S(2)}, u32[]{:S(2)}) collective-permute-start(bf16[2048,256]{1,0:T(8,128)(2,1)S(1)} %shard_map.120.refs_3_), channel_id=1, source_target_pairs={{0,2},{1,3},{2,4},{3,5},{4,6},{5,7},{6,14},{7,15},{14,12},{15,13},... | collective-permute-start | bytes 3145736 | tf_op jit(solution)/shard_map/ppermute | solution.py:257
  169.4 24.5 %collective-permute-start.15 = (bf16[2048,256]{1,0:T(8,128)(2,1)S(1)}, bf16[2048,256]{1,0:T(8,128)(2,1)S(1)}, u32[]{:S(2)}, u32[]{:S(2)}) collective-permute-start(bf16[2048,256]{1,0:T(8,128)(2,1)S(1)} %shard_map.120.refs_3_), channel_id=1, source_target_pairs={{0,8},{1,9},{2,0},{3,1},{4,2},{5,3},{6,4},{7,5},{14,6},{15,7},{12,... | collective-permute-start | bytes 3145736 | tf_op jit(solution)/shard_map/ppermute | solution.py:257
  193.5 25.8 %collective-permute-start.13 = (bf16[2048,256]{1,0:T(8,128)(2,1)}, bf16[2048,256]{1,0:T(8,128)(2,1)S(1)}, u32[]{:S(2)}, u32[]{:S(2)}) collective-permute-start(bf16[2048,256]{1,0:T(8,128)(2,1)} %collective-permute-done.12.refs_4_), channel_id=1, source_target_pairs={{0,2},{1,3},{2,4},{3,5},{4,6},{5,7},{6,14},{7,15},{14,12},{15,13},... | collective-permute-start | bytes 3145736 | tf_op jit(solution)/shard_map/ppermute | solution.py:257
  193.9 25.8 %collective-permute-start.16 = (bf16[2048,256]{1,0:T(8,128)(2,1)S(1)}, bf16[2048,256]{1,0:T(8,128)(2,1)S(1)}, u32[]{:S(2)}, u32[]{:S(2)}) collective-permute-start(bf16[2048,256]{1,0:T(8,128)(2,1)S(1)} %collective-permute-done.15.refs_5_), channel_id=1, source_target_pairs={{0,8},{1,9},{2,0},{3,1},{4,2},{5,3},{6,4},{7,5},{14,6},{15,7},{12,... | collective-permute-start | bytes 3145736 | tf_op jit(solution)/shard_map/ppermute | solution.py:257
  219.2 26.2 %collective-permute-start.26 = (bf16[2048,256]{1,0:T(8,128)(2,1)S(1)}, bf16[2048,256]{1,0:T(8,128)(2,1)S(1)}, u32[]{:S(2)}, u32[]{:S(2)}) collective-permute-start(bf16[2048,256]{1,0:T(8,128)(2,1)S(1)} %copy-done.6), channel_id=1, source_target_pairs={{0,1},{1,0},{2,3},{3,2},{4,5},{5,4},{6,7},{7,6},{14,15},{15,14},{1... | collective-permute-start | bytes 3145736 | tf_op jit(solution)/shard_map/ppermute | solution.py:257
  219.2 25.6 %collective-permute-start.14 = (bf16[2048,256]{1,0:T(8,128)(2,1)S(1)}, bf16[2048,256]{1,0:T(8,128)(2,1)S(1)}, u32[]{:S(2)}, u32[]{:S(2)}) collective-permute-start(bf16[2048,256]{1,0:T(8,128)(2,1)S(1)} %collective-permute-done.13.refs_5_), channel_id=1, source_target_pairs={{0,2},{1,3},{2,4},{3,5},{4,6},{5,7},{6,14},{7,15},{14,12},{15,13},... | collective-permute-start | bytes 3145736 | tf_op jit(solution)/shard_map/ppermute | solution.py:257
  219.7 25.2 %collective-permute-start.17 = (bf16[2048,256]{1,0:T(8,128)(2,1)S(1)}, bf16[2048,256]{1,0:T(8,128)(2,1)S(1)}, u32[]{:S(2)}, u32[]{:S(2)}) collective-permute-start(bf16[2048,256]{1,0:T(8,128)(2,1)S(1)} %collective-permute-done.16.refs_6_), channel_id=1, source_target_pairs={{0,8},{1,9},{2,0},{3,1},{4,2},{5,3},{6,4},{7,5},{14,6},{15,7},{12,... | collective-permute-start | bytes 3145736 | tf_op jit(solution)/shard_map/ppermute | solution.py:257
  238.3 25.8 %collective-permute-start.24 = (bf16[2048,256]{1,0:T(8,128)(2,1)}, bf16[2048,256]{1,0:T(8,128)(2,1)S(1)}, u32[]{:S(2)}, u32[]{:S(2)}) collective-permute-start(bf16[2048,256]{1,0:T(8,128)(2,1)} %collective-permute-done.12.refs_4_), channel_id=1, source_target_pairs={{0,1},{1,0},{2,3},{3,2},{4,5},{5,4},{6,7},{7,6},{14,15},{15,14},{1... | collective-permute-start | bytes 3145736 | tf_op jit(solution)/shard_map/ppermute | solution.py:257
  238.4 26.0 %collective-permute-start.25 = (bf16[2048,256]{1,0:T(8,128)(2,1)S(1)}, bf16[2048,256]{1,0:T(8,128)(2,1)S(1)}, u32[]{:S(2)}, u32[]{:S(2)}) collective-permute-start(bf16[2048,256]{1,0:T(8,128)(2,1)S(1)} %collective-permute-done.15.refs_5_), channel_id=1, source_target_pairs={{0,1},{1,0},{2,3},{3,2},{4,5},{5,4},{6,7},{7,6},{14,15},{15,14},{1... | collective-permute-start | bytes 3145736 | tf_op jit(solution)/shard_map/ppermute | solution.py:257
  244.8 42.1 %collective-permute-start.22 = (bf16[2048,256]{1,0:T(8,128)(2,1)S(1)}, bf16[2048,256]{1,0:T(8,128)(2,1)S(1)}, u32[]{:S(2)}, u32[]{:S(2)}) collective-permute-start(bf16[2048,256]{1,0:T(8,128)(2,1)S(1)} %collective-permute-done.13.refs_5_), channel_id=1, source_target_pairs={{0,1},{1,0},{2,3},{3,2},{4,5},{5,4},{6,7},{7,6},{14,15},{15,14},{1... | collective-permute-start | bytes 3145736 | tf_op jit(solution)/shard_map/ppermute | solution.py:257
  245.0 42.0 %collective-permute-start.23 = (bf16[2048,256]{1,0:T(8,128)(2,1)S(1)}, bf16[2048,256]{1,0:T(8,128)(2,1)S(1)}, u32[]{:S(2)}, u32[]{:S(2)}) collective-permute-start(bf16[2048,256]{1,0:T(8,128)(2,1)S(1)} %collective-permute-done.16.refs_6_), channel_id=1, source_target_pairs={{0,1},{1,0},{2,3},{3,2},{4,5},{5,4},{6,7},{7,6},{14,15},{15,14},{1... | collective-permute-start | bytes 3145736 | tf_op jit(solution)/shard_map/ppermute | solution.py:257
  245.4 19.3 %collective-permute-start.18 = (bf16[2048,256]{1,0:T(8,128)(2,1)S(1)}, bf16[2048,256]{1,0:T(8,128)(2,1)S(1)}, u32[]{:S(2)}, u32[]{:S(2)}) collective-permute-start(bf16[2048,256]{1,0:T(8,128)(2,1)S(1)} %broadcast_select_fusion), channel_id=1, source_target_pairs={{0,2},{1,9},{2,4},{3,1},{4,6},{5,3},{6,14},{7,5},{14,12},{15,7},{1... | collective-permute-start | bytes 3145736 | tf_op jit(solution)/shard_map/ppermute | solution.py:257
  264.2 35.9 %collective-permute-start.20 = (bf16[2048,256]{1,0:T(8,128)(2,1)S(1)}, bf16[2048,256]{1,0:T(8,128)(2,1)S(1)}, u32[]{:S(2)}, u32[]{:S(2)}) collective-permute-start(bf16[2048,256]{1,0:T(8,128)(2,1)S(1)} %collective-permute-done.14.refs_4_), channel_id=1, source_target_pairs={{0,1},{1,0},{2,3},{3,2},{4,5},{5,4},{6,7},{7,6},{14,15},{15,14},{1... | collective-permute-start | bytes 3145736 | tf_op jit(solution)/shard_map/ppermute | solution.py:257
  264.5 35.6 %collective-permute-start.21 = (bf16[2048,256]{1,0:T(8,128)(2,1)S(1)}, bf16[2048,256]{1,0:T(8,128)(2,1)S(1)}, u32[]{:S(2)}, u32[]{:S(2)}) collective-permute-start(bf16[2048,256]{1,0:T(8,128)(2,1)S(1)} %collective-permute-done.17.refs_5_), channel_id=1, source_target_pairs={{0,1},{1,0},{2,3},{3,2},{4,5},{5,4},{6,7},{7,6},{14,15},{15,14},{1... | collective-permute-start | bytes 3145736 | tf_op jit(solution)/shard_map/ppermute | solution.py:257
  264.7 37.4 %collective-permute-start.19 = (bf16[2048,256]{1,0:T(8,128)(2,1)S(1)}, bf16[2048,256]{1,0:T(8,128)(2,1)S(1)}, u32[]{:S(2)}, u32[]{:S(2)}) collective-permute-start(bf16[2048,256]{1,0:T(8,128)(2,1)S(1)} %collective-permute-done.18.refs_0_), channel_id=1, source_target_pairs={{0,1},{1,0},{2,3},{3,2},{4,5},{5,4},{6,7},{7,6},{14,15},{15,14},{1... | collective-permute-start | bytes 3145736 | tf_op jit(solution)/shard_map/ppermute | solution.py:257
  (10 other events, 318.6 us)

commit v2 on v1

--- a/solution.py
+++ b/solution.py
@@ -94,6 +94,49 @@
         compiler_params=params(20),
         cost_estimate=cost(4 * nb * rows * CB * f, 4 * (rows + nb * CB) * f + 4 * rows * nb * CB),
     )(place, dg, du, wg, wu, *after)
+
+
+def both_kernel(nb, place, dg, du, wg, wu, *rest):
+    other, own = rest[-2:]
+    part = 1024
+
+    @pl.loop(0, own.shape[0] // part)
+    def _(i):
+        r = pl.ds(pl.multiple_of(i * part, part), part)
+        t = lax.dot_general(dg[r, :], wg[...], NT, preferred_element_type=F32)
+        t = t + lax.dot_general(du[r, :], wu[...], NT, preferred_element_type=F32)
+
+        @pl.when(pl.program_id(0) < nb)
+        def _():
+            other[r, :] = t.astype(BF16)
+
+        @pl.when(pl.program_id(0) >= nb)
+        def _():
+            own[r, :] = t
+
+
+def both_terms(place, offsets, dg, du, wg, wu, after=()):
+    nb = len(offsets)
+    rows, f = dg.shape
+    lhs = pl.BlockSpec((rows, f), lambda j, p: (0, 0), pipeline_mode=pl.Buffered(1))
+    rhs = pl.BlockSpec(
+        (CB, f), lambda j, p: (column(p, pick(offsets, lax.rem(j, nb)), jnp.where(j < nb, 1 - p[1], p[1])), 0)
+    )
+    return pl.pallas_call(
+        functools.partial(both_kernel, nb),
+        grid_spec=pltpu.PrefetchScalarGridSpec(
+            num_scalar_prefetch=1,
+            grid=(2 * nb,),
+            in_specs=[lhs, lhs, rhs, rhs] + [ANY] * len(after),
+            out_specs=[
+                pl.BlockSpec((rows, CB), lambda j, p: (0, jnp.minimum(j, nb - 1))),
+                pl.BlockSpec((rows, CB), lambda j, p: (0, jnp.maximum(j - nb, 0))),
+            ],
+        ),
+        out_shape=[jax.ShapeDtypeStruct((rows, nb * CB), BF16), jax.ShapeDtypeStruct((rows, nb * CB), F32)],
+        compiler_params=params(22),
+        cost_estimate=cost(8 * nb * rows * CB * f, 4 * (rows + 2 * nb * CB) * f + 6 * rows * nb * CB),
+    )(place, *(dg, du, wg, wu), *after)
 
 
 def add_kernel(only, place, *refs):
@@ -269,6 +312,9 @@
 
         def stage(o, *after):
             given = (place, o, d_gate, d_up, w_gate, w_up, after)
+            if o[0] < 3:
+                other, own = both_terms(*given)
+                return send(other, swap), own
             other = terms(False, *given)
             other = send(other, swap)
             return other, terms(True, *given)
@@ -283,30 +329,30 @@
         other, own = stage((4,))
         far = add(place, own, other, 0)
         other, own = stage((3, -3), far)
-        dw_down = ()
+        dw = ()
         got_r = got_l = send(far, apart)
         for o, then in ((3, (2, -2)), (2, (1, -1)), (1, (0,))):
             to_r = add(place, own, other, 0, got_r, only=0 if o == 3 else None)
             to_l = add(place, own, other, 1, got_l, only=1 if o == 3 else None)
             other, own = stage(then, to_r, to_l)
             got_r, got_l = send(to_r, right), send(to_l, left)
-            first, count = {3: (0, 1), 2: (1, 1), 1: (2, 2)}[o]
-            dw_down = gradients("down", first, count, dw_down)
+            if o != 2:
+                first, count = {3: (0, 1), 1: (1, 3)}[o]
+                dw = gradients("pair", first, count, dw)
         done = add(place, own, other, 0, got_r, got_l)
 
         a1 = [send(done, right), send(done, left)]
         b0 = [send(done, swap)]
-        *dw, dx = gradients("pair", 0, 3, (), None, [done], [(0, True)])
+        *dw, dx = gradients("pair", 4, 4, dw, None, [done], [(0, True)])
         a2 = [send(a1[0], right), send(a1[1], left)]
         b1 = [send(v, swap) for v in a1]
-        *dw, dx = gradients("pair", 3, 3, dw, dx, b0 + a1, [(0, False)] + both(1)[0])
+        dw_down, dx = gradients("down", 0, 5, (), dx, b0 + a1, [(0, False)] + both(1)[0])
         a3 = [send(a2[0], right), send(a2[1], left)]
         b2 = [send(v, swap) for v in a2]
-        *dw, dx = gradients("pair", 6, 2, dw, dx, b1 + a2, both(1)[1] + both(2)[0])
-        dw_down = gradients("down", 4, 1, dw_down, None, (), (), (dx,))
+        dw_down, dx = gradients("down", 5, 3, (dw_down,), dx, b1 + a2, both(1)[1] + both(2)[0])
         last = send(jnp.where(core == 0, a3[0], a3[1]), apart)
         b3 = [send(v, swap) for v in a3]
-        dw_down, dx = gradients("down", 5, 3, dw_down, dx, b2 + a3, both(2)[1] + both(3)[0])
+        dx = put(place, dx, b2 + a3, both(2)[1] + both(3)[0])
         dx = put(place, dx, b3, both(3)[1])
         dx = put(place, dx, [last, send(last, swap)], [(4, True), (4, False)])
         return dx, *dw, dw_down

time: 305 us -> 319 us (1.046)
  waiting for transfers between devices: 87.2 us -> 113 us
  Pallas kernels: 196 us -> 180 us
  local copies, waits for them, and re-layouts: 0.03 us -> 4.41 us
    pallas_call x10 -> x4, Pallas kernels: 61.5 us -> 23.9 us  [terms(): pl.pallas_call(term_kernel, grid_spec=pltpu.PrefetchScalarGridSpec(num_sc...]
    pallas_call x0 -> x3, Pallas kernels: none -> 33.7 us  [both_terms(): pl.pallas_call(functools.partial(both_kernel, nb), grid_spec=pltpu.Prefet...]
    ppermute x27, waiting for transfers between devices: 87.2 us -> 113 us  [send(): return lax.ppermute(v, 'tp', pairs)]
    pallas_call x8 -> x5, Pallas kernels: 93 us -> 77.4 us  [weights(): pl.pallas_call(functools.partial(weights_kernel, kind, count, len(given)...]
    unnamed x14 -> x16, local copies, waits for them, and re-layouts: 0.03 us -> 4.41 us
    pallas_call x2 -> x3, Pallas kernels: 4.09 us -> 7.01 us  [put(): pl.pallas_call(functools.partial(place_kernel, placing, 1), grid_spec=plt...]
  transfers between devices with their start and end apart: 27 -> 27, of which waited for: 10 -> 12; matrix products, arithmetic and copies ran while one was open for 0% -> 0% of each run, Pallas kernels for 42% -> 30%
where the time goes in v2:
time: 319 us
  Pallas kernels  180 us (56%)
  waiting for transfers between devices  113 us (35%)
  starting transfers between devices  20.5 us (6%)
  local copies, waits for them, and re-layouts  4.41 us (1%)
    ppermute x27, waiting for transfers between devices, send(): return lax.ppermute(v, 'tp', pairs)  113 us
    pallas_call x5, Pallas kernels, weights(): pl.pallas_call(functools.partial(weights_kernel, kind, count, len(given)...  77.4 us
    pallas_call x3, Pallas kernels, both_terms(): pl.pallas_call(functools.partial(both_kernel, nb), grid_spec=pltpu.Prefet...  33.7 us
    pallas_call x1, Pallas kernels, back(): pl.pallas_call(back_kernel, grid=(rows // tile, f // tf), in_specs=[pl.Bl...  28.5 us
    pallas_call x4, Pallas kernels, terms(): pl.pallas_call(term_kernel, grid_spec=pltpu.PrefetchScalarGridSpec(num_sc...  23.9 us
    ppermute x27, starting transfers between devices, send(): return lax.ppermute(v, 'tp', pairs)  20.5 us
    pallas_call x8, Pallas kernels, add(): pl.pallas_call(functools.partial(add_kernel, only), grid_spec=pltpu.Prefe...  9.18 us
    pallas_call x3, Pallas kernels, put(): pl.pallas_call(functools.partial(place_kernel, placing, 1), grid_spec=plt...  7.01 us
  transfers between devices with their start and end apart: 27, of which 12 were waited for; matrix products, arithmetic and copies ran while one was open for 0% of the time, Pallas kernels for 30%

profile of v2, /device:TPU:0, one launch (start us, length us, event | category | flops | bytes accessed | tf_op | source)
XLA Modules:
  0.0 318.9 jit_solution(8758868094118508321)
XLA Ops:
  0.7 28.5 %shard_map.102 = (bf16[2048,1024]{1,0:T(8,128)(2,1)S(1)}, bf16[2048,1024]{1,0:T(8,128)(2,1)S(1)}, bf16[2048,1024]{1,0:T(8,128)(2,1)S(1)}) custom-call(bf16[2048,4096]{1,0:T(8,128)(2,1)} %refs_1_.3, bf16[1024,4096]{1,0:T(8,128)(2,1)} %w_down.1, bf16[2048,1024]{1,0:T(8,128)(2,1)} %gate.1, bf16[2048,1024]{1,0:T(8,128)(2,1)} %up.1), custom_call_target="tpu_custom_call" | custom-call | flops 17179869184 | bytes 46137344 | tf_op jit(solution)/shard_map/pallas_call | solution.py:43
  29.3 5.1 %shard_map.104 = bf16[2048,256]{1,0:T(8,128)(2,1)S(1)} custom-call(s32[2]{0:T(128)S(1)} %pad_add_fusion.place, bf16[2048,1024]{1,0:T(8,128)(2,1)S(1)} %get-tuple-element.24.dg.refs_1_, bf16[2048,1024]{1,0:T(8,128)(2,1)S(1)} %get-tuple-element.25.du.refs_2_, bf16[4096,1024]{1,0:T(8,128)(2,1)} %wg.13, bf16[4096,1024]{1,0:T(8,128)(2,1)} %wu.13), custom_call_target="tpu_custom_call" | custom-call | flops 2147483648 | bytes 11534336 | tf_op jit(solution)/shard_map/pallas_call | solution.py:85
  35.0 4.3 %shard_map.103.refs_0_ = f32[2048,256]{1,0:T(8,128)S(1)} custom-call(s32[2]{0:T(128)S(1)} %pad_add_fusion.place, bf16[2048,1024]{1,0:T(8,128)(2,1)S(1)} %get-tuple-element.24.dg.refs_1_, bf16[2048,1024]{1,0:T(8,128)(2,1)S(1)} %get-tuple-element.25.du.refs_2_, bf16[4096,1024]{1,0:T(8,128)(2,1)} %wg.13, bf16[4096,1024]{1,0:T(8,128)(2,1)} %wu.13), custom_call_target="tpu_custom_call" | custom-call | flops 2147483648 | bytes 11534336 | tf_op jit(solution)/shard_map/pallas_call | solution.py:85
  40.1 7.1 %shard_map.107 = bf16[2048,512]{1,0:T(8,128)(2,1)S(1)} custom-call(s32[2]{0:T(128)S(1)} %pad_add_fusion.place, bf16[2048,1024]{1,0:T(8,128)(2,1)S(1)} %get-tuple-element.24.dg.refs_1_, bf16[2048,1024]{1,0:T(8,128)(2,1)S(1)} %get-tuple-element.25.du.refs_2_, bf16[4096,1024]{1,0:T(8,128)(2,1)} %wg.13, bf16[4096,1024]{1,0:T(8,128)(2,1)} %wu.13, ...), custom_call_target="tpu_custom_call" | custom-call | flops 4294967296 | bytes 14680064 | tf_op jit(solution)/shard_map/pallas_call | solution.py:85
  47.3 3.1 collective-permute-start.2
  50.4 7.3 %shard_map.106.refs_0_ = f32[2048,512]{1,0:T(8,128)S(1)} custom-call(s32[2]{0:T(128)S(1)} %pad_add_fusion.place, bf16[2048,1024]{1,0:T(8,128)(2,1)S(1)} %get-tuple-element.24.dg.refs_1_, bf16[2048,1024]{1,0:T(8,128)(2,1)S(1)} %get-tuple-element.25.du.refs_2_, bf16[4096,1024]{1,0:T(8,128)(2,1)} %wg.13, bf16[4096,1024]{1,0:T(8,128)(2,1)} %wu.13, ...), custom_call_target="tpu_custom_call" | custom-call | flops 4294967296 | bytes 14680064 | tf_op jit(solution)/shard_map/pallas_call | solution.py:85
  57.7 5.4 %collective-permute-done.2.refs_2_ = bf16[2048,256]{1,0:T(8,128)(2,1)S(1)} collective-permute-done((bf16[2048,256]{1,0:T(8,128)(2,1)S(1)}, bf16[2048,256]{1,0:T(8,128)(2,1)S(1)}, u32[]{:S(2)}, u32[]{:S(2)}) %collective-permute-start.2) | collective-permute-done | bytes 1048608 | tf_op jit(solution)/shard_map/ppermute | solution.py:300
  65.6 13.2 %shard_map.110 = (bf16[2048,512]{1,0:T(8,128)(2,1)S(1)}, f32[2048,512]{1,0:T(8,128)S(1)}) custom-call(s32[2]{0:T(128)S(1)} %pad_add_fusion.place, bf16[2048,1024]{1,0:T(8,128)(2,1)S(1)} %get-tuple-element.24.dg.refs_1_, bf16[2048,1024]{1,0:T(8,128)(2,1)S(1)} %get-tuple-element.25.du.refs_2_, bf16[4096,1024]{1,0:T(8,128)(2,1)} %wg.13, ...), custom_call_target="tpu_custom_call" | custom-call | flops 8589934592 | bytes 18874368 | tf_op jit(solution)/shard_map/pallas_call | solution.py:125
  81.1 23.7 %collective-permute-done.5.refs_2_ = bf16[2048,256]{1,0:T(8,128)(2,1)S(1)} collective-permute-done((bf16[2048,256]{1,0:T(8,128)(2,1)S(1)}, bf16[2048,256]{1,0:T(8,128)(2,1)S(1)}, u32[]{:S(2)}, u32[]{:S(2)}) %collective-permute-start.5) | collective-permute-done | bytes 1048608 | tf_op jit(solution)/shard_map/ppermute | solution.py:300
  107.4 13.2 %shard_map.113 = (bf16[2048,512]{1,0:T(8,128)(2,1)S(1)}, f32[2048,512]{1,0:T(8,128)S(1)}) custom-call(s32[2]{0:T(128)S(1)} %pad_add_fusion.place, bf16[2048,1024]{1,0:T(8,128)(2,1)S(1)} %get-tuple-element.24.dg.refs_1_, bf16[2048,1024]{1,0:T(8,128)(2,1)S(1)} %get-tuple-element.25.du.refs_2_, bf16[4096,1024]{1,0:T(8,128)(2,1)} %wg.13, ...), custom_call_target="tpu_custom_call" | custom-call | flops 8589934592 | bytes 18874368 | tf_op jit(solution)/shard_map/pallas_call | solution.py:125
  122.8 23.5 %collective-permute-done.8.refs_2_ = bf16[2048,256]{1,0:T(8,128)(2,1)S(1)} collective-permute-done((bf16[2048,256]{1,0:T(8,128)(2,1)S(1)}, bf16[2048,256]{1,0:T(8,128)(2,1)S(1)}, u32[]{:S(2)}, u32[]{:S(2)}) %collective-permute-start.8) | collective-permute-done | bytes 1048608 | tf_op jit(solution)/shard_map/ppermute | solution.py:300
  148.8 7.2 %shard_map.116 = (bf16[2048,256]{1,0:T(8,128)(2,1)S(1)}, f32[2048,256]{1,0:T(8,128)S(1)}) custom-call(s32[2]{0:T(128)S(1)} %pad_add_fusion.place, bf16[2048,1024]{1,0:T(8,128)(2,1)S(1)} %get-tuple-element.24.dg.refs_1_, bf16[2048,1024]{1,0:T(8,128)(2,1)S(1)} %get-tuple-element.25.du.refs_2_, bf16[4096,1024]{1,0:T(8,128)(2,1)} %wg.13, ...), custom_call_target="tpu_custom_call" | custom-call | flops 4294967296 | bytes 13631488 | tf_op jit(solution)/shard_map/pallas_call | solution.py:125
  158.8 22.9 %collective-permute-done.11.refs_3_ = bf16[2048,256]{1,0:T(8,128)(2,1)S(1)} collective-permute-done((bf16[2048,256]{1,0:T(8,128)(2,1)S(1)}, bf16[2048,256]{1,0:T(8,128)(2,1)S(1)}, u32[]{:S(2)}, u32[]{:S(2)}) %collective-permute-start.11) | collective-permute-done | bytes 1048608 | tf_op jit(solution)/shard_map/ppermute | solution.py:300
  186.2 22.3 %collective-permute-done.12.refs_3_ = bf16[2048,256]{1,0:T(8,128)(2,1)S(1)} collective-permute-done((bf16[2048,256]{1,0:T(8,128)(2,1)S(1)}, bf16[2048,256]{1,0:T(8,128)(2,1)S(1)}, u32[]{:S(2)}, u32[]{:S(2)}) %collective-permute-start.12) | collective-permute-done | bytes 1048608 | tf_op jit(solution)/shard_map/ppermute | solution.py:300
  210.6 2.2 copy-done.1
  215.0 7.6 %shard_map.118 = (bf16[4096,1024]{1,0:T(8,128)(2,1)}, bf16[4096,1024]{1,0:T(8,128)(2,1)}) custom-call(s32[2]{0:T(128)S(1)} %pad_add_fusion.place, bf16[2048,4096]{1,0:T(8,128)(2,1)} %refs_0_.5, bf16[2048,1024]{1,0:T(8,128)(2,1)S(1)} %copy-done.1, bf16[2048,1024]{1,0:T(8,128)(2,1)S(1)} %copy-done.4), custom_call_target="tpu_custom_call" | custom-call | flops 4294967296 | bytes 12582912 | tf_op jit(solution)/shard_map/pallas_call | solution.py:245
  222.6 9.6 %collective-permute-done.13.refs_4_ = bf16[2048,256]{1,0:T(8,128)(2,1)S(1)} collective-permute-done((bf16[2048,256]{1,0:T(8,128)(2,1)S(1)}, bf16[2048,256]{1,0:T(8,128)(2,1)S(1)}, u32[]{:S(2)}, u32[]{:S(2)}) %collective-permute-start.13) | collective-permute-done | bytes 1048608 | tf_op jit(solution)/shard_map/ppermute | solution.py:300
  234.2 17.0 %shard_map.119 = (bf16[4096,1024]{1,0:T(8,128)(2,1)}, bf16[4096,1024]{1,0:T(8,128)(2,1)}) custom-call(s32[2]{0:T(128)S(1)} %pad_add_fusion.place, bf16[2048,4096]{1,0:T(8,128)(2,1)} %refs_0_.5, bf16[2048,1024]{1,0:T(8,128)(2,1)S(1)} %copy-done.1, bf16[2048,1024]{1,0:T(8,128)(2,1)S(1)} %copy-done.4, ...), custom_call_target="tpu_custom_call", output_to_operand_aliasing={{0}: (4, {}), {1}: (5, {})} | custom-call | flops 12884901888 | bytes 20971520 | tf_op jit(solution)/shard_map/pallas_call | solution.py:245
  251.8 3.2 collective-permute-done.14.refs_2_
  255.3 2.4 collective-permute-start.18
  257.6 21.5 %shard_map.120 = (bf16[4096,1024]{1,0:T(8,128)(2,1)}, bf16[4096,1024]{1,0:T(8,128)(2,1)}, bf16[2048,4096]{1,0:T(8,128)(2,1)}) custom-call(s32[2]{0:T(128)S(1)} %pad_add_fusion.place, bf16[2048,4096]{1,0:T(8,128)(2,1)} %refs_0_.5, bf16[2048,1024]{1,0:T(8,128)(2,1)S(1)} %copy-done.2, ...), custom_call_target="tpu_custom_call", output_to_operand_aliasing={{0}: (5, {}), {1}: (6, {})} | custom-call | flops 17179869184 | bytes 25165824 | tf_op jit(solution)/shard_map/pallas_call | solution.py:245
  280.4 18.1 %shard_map.121 = (bf16[1024,4096]{1,0:T(8,128)(2,1)}, bf16[2048,4096]{1,0:T(8,128)(2,1)}) custom-call(s32[2]{0:T(128)S(1)} %pad_add_fusion.place, bf16[2048,1024]{1,0:T(8,128)(2,1)} %copy-done.5, bf16[2048,4096]{1,0:T(8,128)(2,1)} %refs_1_.3, bf16[2048,256]{1,0:T(8,128)(2,1)S(1)} %collective-permute-done.26.refs_2_, ...), custom_call_target="tpu_custom_call", output_to_operand_aliasing={{1}: (6, {})} | custom-call | flops 10737418240 | bytes 29360128 | tf_op jit(solution)/shard_map/pallas_call | solution.py:245
  298.5 13.1 %shard_map.122 = (bf16[1024,4096]{1,0:T(8,128)(2,1)}, bf16[2048,4096]{1,0:T(8,128)(2,1)}) custom-call(s32[2]{0:T(128)S(1)} %pad_add_fusion.place, bf16[2048,1024]{1,0:T(8,128)(2,1)} %copy-done.5, bf16[2048,4096]{1,0:T(8,128)(2,1)} %refs_1_.3, bf16[2048,256]{1,0:T(8,128)(2,1)S(1)} %collective-permute-done.24.refs_2_, ...), custom_call_target="tpu_custom_call", output_to_operand_aliasing={{0}: (7, {}), {1}: (8, {})} | custom-call | flops 6442450944 | bytes 20971520 | tf_op jit(solution)/shard_map/pallas_call | solution.py:245
  311.7 2.9 shard_map.123.refs_2_
  (72 shorter events, 33.2 us)
Async XLA Ops:
  47.2 15.8 %collective-permute-start.1 = (bf16[2048,512]{1,0:T(8,128)(2,1)S(1)}, bf16[2048,512]{1,0:T(8,128)(2,1)S(1)}, u32[]{:S(2)}, u32[]{:S(2)}) collective-permute-start(bf16[2048,512]{1,0:T(8,128)(2,1)S(1)} %shard_map.107), channel_id=1, source_target_pairs={{0,1},{1,0},{2,3},{3,2},{4,5},{5,4},{6,7},{7,6},{14,15},{15,14},{1... | collective-permute-start | bytes 6291464 | tf_op jit(solution)/shard_map/ppermute | solution.py:300
  78.8 26.0 %collective-permute-start.3 = (bf16[2048,512]{1,0:T(8,128)(2,1)S(1)}, bf16[2048,512]{1,0:T(8,128)(2,1)S(1)}, u32[]{:S(2)}, u32[]{:S(2)}) collective-permute-start(bf16[2048,512]{1,0:T(8,128)(2,1)S(1)} %get-tuple-element.27), channel_id=1, source_target_pairs={{0,1},{1,0},{2,3},{3,2},{4,5},{5,4},{6,7},{7,6},{14,15},{15,14},{1... | collective-permute-start | bytes 6291464 | tf_op jit(solution)/shard_map/ppermute | solution.py:300
  78.9 25.9 %collective-permute-start.5 = (bf16[2048,256]{1,0:T(8,128)(2,1)S(1)}, bf16[2048,256]{1,0:T(8,128)(2,1)S(1)}, u32[]{:S(2)}, u32[]{:S(2)}) collective-permute-start(bf16[2048,256]{1,0:T(8,128)(2,1)S(1)} %shard_map.109.rest_1_), channel_id=1, source_target_pairs={{0,8},{1,9},{2,0},{3,1},{4,2},{5,3},{6,4},{7,5},{14,6},{15,7},{12,... | collective-permute-start | bytes 3145736 | tf_op jit(solution)/shard_map/ppermute | solution.py:300
  81.0 25.2 %collective-permute-start.4 = (bf16[2048,256]{1,0:T(8,128)(2,1)S(1)}, bf16[2048,256]{1,0:T(8,128)(2,1)S(1)}, u32[]{:S(2)}, u32[]{:S(2)}) collective-permute-start(bf16[2048,256]{1,0:T(8,128)(2,1)S(1)} %shard_map.108.rest_0_), channel_id=1, source_target_pairs={{0,2},{1,3},{2,4},{3,5},{4,6},{5,7},{6,14},{7,15},{14,12},{15,13},... | collective-permute-start | bytes 3145736 | tf_op jit(solution)/shard_map/ppermute | solution.py:300
  120.6 25.6 %collective-permute-start.6 = (bf16[2048,512]{1,0:T(8,128)(2,1)S(1)}, bf16[2048,512]{1,0:T(8,128)(2,1)S(1)}, u32[]{:S(2)}, u32[]{:S(2)}) collective-permute-start(bf16[2048,512]{1,0:T(8,128)(2,1)S(1)} %get-tuple-element.29), channel_id=1, source_target_pairs={{0,1},{1,0},{2,3},{3,2},{4,5},{5,4},{6,7},{7,6},{14,15},{15,14},{1... | collective-permute-start | bytes 6291464 | tf_op jit(solution)/shard_map/ppermute | solution.py:300
  120.7 25.6 %collective-permute-start.8 = (bf16[2048,256]{1,0:T(8,128)(2,1)S(1)}, bf16[2048,256]{1,0:T(8,128)(2,1)S(1)}, u32[]{:S(2)}, u32[]{:S(2)}) collective-permute-start(bf16[2048,256]{1,0:T(8,128)(2,1)S(1)} %shard_map.112.rest_1_), channel_id=1, source_target_pairs={{0,8},{1,9},{2,0},{3,1},{4,2},{5,3},{6,4},{7,5},{14,6},{15,7},{12,... | collective-permute-start | bytes 3145736 | tf_op jit(solution)/shard_map/ppermute | solution.py:300
  122.4 25.2 %collective-permute-start.7 = (bf16[2048,256]{1,0:T(8,128)(2,1)S(1)}, bf16[2048,256]{1,0:T(8,128)(2,1)S(1)}, u32[]{:S(2)}, u32[]{:S(2)}) collective-permute-start(bf16[2048,256]{1,0:T(8,128)(2,1)S(1)} %shard_map.111.rest_0_), channel_id=1, source_target_pairs={{0,2},{1,3},{2,4},{3,5},{4,6},{5,7},{6,14},{7,15},{14,12},{15,13},... | collective-permute-start | bytes 3145736 | tf_op jit(solution)/shard_map/ppermute | solution.py:300
  156.1 25.6 %collective-permute-start.11 = (bf16[2048,256]{1,0:T(8,128)(2,1)S(1)}, bf16[2048,256]{1,0:T(8,128)(2,1)S(1)}, u32[]{:S(2)}, u32[]{:S(2)}) collective-permute-start(bf16[2048,256]{1,0:T(8,128)(2,1)S(1)} %shard_map.115.rest_1_), channel_id=1, source_target_pairs={{0,8},{1,9},{2,0},{3,1},{4,2},{5,3},{6,4},{7,5},{14,6},{15,7},{12,... | collective-permute-start | bytes 3145736 | tf_op jit(solution)/shard_map/ppermute | solution.py:300
  157.7 25.2 %collective-permute-start.10 = (bf16[2048,256]{1,0:T(8,128)(2,1)S(1)}, bf16[2048,256]{1,0:T(8,128)(2,1)S(1)}, u32[]{:S(2)}, u32[]{:S(2)}) collective-permute-start(bf16[2048,256]{1,0:T(8,128)(2,1)S(1)} %shard_map.114.rest_0_), channel_id=1, source_target_pairs={{0,2},{1,3},{2,4},{3,5},{4,6},{5,7},{6,14},{7,15},{14,12},{15,13},... | collective-permute-start | bytes 3145736 | tf_op jit(solution)/shard_map/ppermute | solution.py:300
  184.1 24.4 %collective-permute-start.12 = (bf16[2048,256]{1,0:T(8,128)(2,1)S(1)}, bf16[2048,256]{1,0:T(8,128)(2,1)S(1)}, u32[]{:S(2)}, u32[]{:S(2)}) collective-permute-start(bf16[2048,256]{1,0:T(8,128)(2,1)S(1)} %shard_map.117.refs_3_), channel_id=1, source_target_pairs={{0,2},{1,3},{2,4},{3,5},{4,6},{5,7},{6,14},{7,15},{14,12},{15,13},... | collective-permute-start | bytes 3145736 | tf_op jit(solution)/shard_map/ppermute | solution.py:300
  184.6 24.4 %collective-permute-start.15 = (bf16[2048,256]{1,0:T(8,128)(2,1)S(1)}, bf16[2048,256]{1,0:T(8,128)(2,1)}, u32[]{:S(2)}, u32[]{:S(2)}) collective-permute-start(bf16[2048,256]{1,0:T(8,128)(2,1)S(1)} %shard_map.117.refs_3_), channel_id=1, source_target_pairs={{0,8},{1,9},{2,0},{3,1},{4,2},{5,3},{6,4},{7,5},{14,6},{15,7},{12,... | collective-permute-start | bytes 3145736 | tf_op jit(solution)/shard_map/ppermute | solution.py:300
  208.6 23.6 %collective-permute-start.13 = (bf16[2048,256]{1,0:T(8,128)(2,1)S(1)}, bf16[2048,256]{1,0:T(8,128)(2,1)S(1)}, u32[]{:S(2)}, u32[]{:S(2)}) collective-permute-start(bf16[2048,256]{1,0:T(8,128)(2,1)S(1)} %collective-permute-done.12.refs_3_), channel_id=1, source_target_pairs={{0,2},{1,3},{2,4},{3,5},{4,6},{5,7},{6,14},{7,15},{14,12},{15,13},... | collective-permute-start | bytes 3145736 | tf_op jit(solution)/shard_map/ppermute | solution.py:300
  209.0 23.6 %collective-permute-start.16 = (bf16[2048,256]{1,0:T(8,128)(2,1)}, bf16[2048,256]{1,0:T(8,128)(2,1)S(1)}, u32[]{:S(2)}, u32[]{:S(2)}) collective-permute-start(bf16[2048,256]{1,0:T(8,128)(2,1)} %collective-permute-done.15.refs_4_), channel_id=1, source_target_pairs={{0,8},{1,9},{2,0},{3,1},{4,2},{5,3},{6,4},{7,5},{14,6},{15,7},{12,... | collective-permute-start | bytes 3145736 | tf_op jit(solution)/shard_map/ppermute | solution.py:300
  232.2 22.8 %collective-permute-start.14 = (bf16[2048,256]{1,0:T(8,128)(2,1)S(1)}, bf16[2048,256]{1,0:T(8,128)(2,1)S(1)}, u32[]{:S(2)}, u32[]{:S(2)}) collective-permute-start(bf16[2048,256]{1,0:T(8,128)(2,1)S(1)} %collective-permute-done.13.refs_4_), channel_id=1, source_target_pairs={{0,2},{1,3},{2,4},{3,5},{4,6},{5,7},{6,14},{7,15},{14,12},{15,13},... | collective-permute-start | bytes 3145736 | tf_op jit(solution)/shard_map/ppermute | solution.py:300
  232.7 22.5 %collective-permute-start.17 = (bf16[2048,256]{1,0:T(8,128)(2,1)S(1)}, bf16[2048,256]{1,0:T(8,128)(2,1)S(1)}, u32[]{:S(2)}, u32[]{:S(2)}) collective-permute-start(bf16[2048,256]{1,0:T(8,128)(2,1)S(1)} %collective-permute-done.16.refs_5_), channel_id=1, source_target_pairs={{0,8},{1,9},{2,0},{3,1},{4,2},{5,3},{6,4},{7,5},{14,6},{15,7},{12,... | collective-permute-start | bytes 3145736 | tf_op jit(solution)/shard_map/ppermute | solution.py:300
  251.2 28.1 %collective-permute-start.26 = (bf16[2048,256]{1,0:T(8,128)(2,1)S(1)}, bf16[2048,256]{1,0:T(8,128)(2,1)S(1)}, u32[]{:S(2)}, u32[]{:S(2)}) collective-permute-start(bf16[2048,256]{1,0:T(8,128)(2,1)S(1)} %copy-done.7), channel_id=1, source_target_pairs={{0,1},{1,0},{2,3},{3,2},{4,5},{5,4},{6,7},{7,6},{14,15},{15,14},{1... | collective-permute-start | bytes 3145736 | tf_op jit(solution)/shard_map/ppermute | solution.py:300
  251.2 28.6 %collective-permute-start.24 = (bf16[2048,256]{1,0:T(8,128)(2,1)S(1)}, bf16[2048,256]{1,0:T(8,128)(2,1)S(1)}, u32[]{:S(2)}, u32[]{:S(2)}) collective-permute-start(bf16[2048,256]{1,0:T(8,128)(2,1)S(1)} %collective-permute-done.12.refs_3_), channel_id=1, source_target_pairs={{0,1},{1,0},{2,3},{3,2},{4,5},{5,4},{6,7},{7,6},{14,15},{15,14},{1... | collective-permute-start | bytes 3145736 | tf_op jit(solution)/shard_map/ppermute | solution.py:300
  251.7 28.2 %collective-permute-start.25 = (bf16[2048,256]{1,0:T(8,128)(2,1)}, bf16[2048,256]{1,0:T(8,128)(2,1)S(1)}, u32[]{:S(2)}, u32[]{:S(2)}) collective-permute-start(bf16[2048,256]{1,0:T(8,128)(2,1)} %collective-permute-done.15.refs_4_), channel_id=1, source_target_pairs={{0,1},{1,0},{2,3},{3,2},{4,5},{5,4},{6,7},{7,6},{14,15},{15,14},{1... | collective-permute-start | bytes 3145736 | tf_op jit(solution)/shard_map/ppermute | solution.py:300
  255.3 25.0 %collective-permute-start.18 = (bf16[2048,256]{1,0:T(8,128)(2,1)S(1)}, bf16[2048,256]{1,0:T(8,128)(2,1)S(1)}, u32[]{:S(2)}, u32[]{:S(2)}) collective-permute-start(bf16[2048,256]{1,0:T(8,128)(2,1)S(1)} %broadcast_select_fusion), channel_id=1, source_target_pairs={{0,2},{1,9},{2,4},{3,1},{4,6},{5,3},{6,14},{7,5},{14,12},{15,7},{1... | collective-permute-start | bytes 3145736 | tf_op jit(solution)/shard_map/ppermute | solution.py:300
  279.2 32.4 %collective-permute-start.22 = (bf16[2048,256]{1,0:T(8,128)(2,1)S(1)}, bf16[2048,256]{1,0:T(8,128)(2,1)S(1)}, u32[]{:S(2)}, u32[]{:S(2)}) collective-permute-start(bf16[2048,256]{1,0:T(8,128)(2,1)S(1)} %collective-permute-done.13.refs_4_), channel_id=1, source_target_pairs={{0,1},{1,0},{2,3},{3,2},{4,5},{5,4},{6,7},{7,6},{14,15},{15,14},{1... | collective-permute-start | bytes 3145736 | tf_op jit(solution)/shard_map/ppermute | solution.py:300
  279.3 32.4 %collective-permute-start.23 = (bf16[2048,256]{1,0:T(8,128)(2,1)S(1)}, bf16[2048,256]{1,0:T(8,128)(2,1)S(1)}, u32[]{:S(2)}, u32[]{:S(2)}) collective-permute-start(bf16[2048,256]{1,0:T(8,128)(2,1)S(1)} %collective-permute-done.16.refs_5_), channel_id=1, source_target_pairs={{0,1},{1,0},{2,3},{3,2},{4,5},{5,4},{6,7},{7,6},{14,15},{15,14},{1... | collective-permute-start | bytes 3145736 | tf_op jit(solution)/shard_map/ppermute | solution.py:300
  279.8 34.8 %collective-permute-start.20 = (bf16[2048,256]{1,0:T(8,128)(2,1)S(1)}, bf16[2048,256]{1,0:T(8,128)(2,1)S(1)}, u32[]{:S(2)}, u32[]{:S(2)}) collective-permute-start(bf16[2048,256]{1,0:T(8,128)(2,1)S(1)} %collective-permute-done.14.refs_2_), channel_id=1, source_target_pairs={{0,1},{1,0},{2,3},{3,2},{4,5},{5,4},{6,7},{7,6},{14,15},{15,14},{1... | collective-permute-start | bytes 3145736 | tf_op jit(solution)/shard_map/ppermute | solution.py:300
  279.9 34.7 %collective-permute-start.21 = (bf16[2048,256]{1,0:T(8,128)(2,1)S(1)}, bf16[2048,256]{1,0:T(8,128)(2,1)S(1)}, u32[]{:S(2)}, u32[]{:S(2)}) collective-permute-start(bf16[2048,256]{1,0:T(8,128)(2,1)S(1)} %collective-permute-done.17.refs_3_), channel_id=1, source_target_pairs={{0,1},{1,0},{2,3},{3,2},{4,5},{5,4},{6,7},{7,6},{14,15},{15,14},{1... | collective-permute-start | bytes 3145736 | tf_op jit(solution)/shard_map/ppermute | solution.py:300
  280.3 36.4 %collective-permute-start.19 = (bf16[2048,256]{1,0:T(8,128)(2,1)S(1)}, bf16[2048,256]{1,0:T(8,128)(2,1)S(1)}, u32[]{:S(2)}, u32[]{:S(2)}) collective-permute-start(bf16[2048,256]{1,0:T(8,128)(2,1)S(1)} %collective-permute-done.18.refs_0_), channel_id=1, source_target_pairs={{0,1},{1,0},{2,3},{3,2},{4,5},{5,4},{6,7},{7,6},{14,15},{15,14},{1... | collective-permute-start | bytes 3145736 | tf_op jit(solution)/shard_map/ppermute | solution.py:300
  (11 other events, 337.4 us)
